TPU v7x, 32 devices: a whole 2x2x4 slice. The times are simulated.
32 devices in a mesh: grp: 2 (over x), blk: 8 (over z, y), vec: 2 (over core).
Axes of the slice: x: 2, y: 2, z: 4, core: 2. Of those that a mesh axis runs over, the one named last changes fastest.
Arguments:
- trial: bfloat16 [20480, 32], P(('grp', 'blk', 'vec')), may hold values from -6 to 6
- energy_gap: float32 [20480], P(('grp', 'blk', 'vec')), may hold values from 0.5 to 2.5
- coulomb_factors: bfloat16 [4096, 20480], P('blk'), may hold values from -0.0390625 to 0.0390625
- occ_values: bfloat16 [80, 40, 512], P('blk'), may hold values from -1 to 1
- vir_values: bfloat16 [80, 512, 512], P('blk'), may hold values from -1 to 1
- kernel: float32 [80, 512], P('blk'), may hold values from 0.2 to 2
- live_points: int32 [80], P('blk'), may hold values from 64 to 512
Outputs:
- sigma: bfloat16 [20480, 32], P(('grp', 'blk', 'vec'))
All inputs are finite; a program needn't handle non-finite values.
Results may differ from a plain program's by a relative error of at most 0.0029.
Values may be sent and summed in bfloat16 or wider, within the bound.
A program may use at most 64 MiB of HBM per device.

v0:
```python
import jax
import jax.numpy as jnp
from jax import lax
from jax.sharding import PartitionSpec as P


def local(trial, energy_gap, coulomb_factors, occ_values, vir_values, kernel, live_points):
    pair_rows = lax.all_to_all(trial, "vec", split_axis=1, concat_axis=0, tiled=True)
    full = lax.all_gather(pair_rows, ("grp", "blk"), axis=0, tiled=True)
    occ_count = occ_values.shape[1]
    batch_size = occ_values.shape[2]
    vir_count = vir_values.shape[2]
    width = full.shape[1]
    batches = occ_values.shape[0]
    rearranged = (
        full.reshape(occ_count, vir_count, width)
        .transpose(1, 0, 2)
        .reshape(vir_count, occ_count * width)
    )
    slots = jnp.arange(batch_size, dtype=jnp.int32)

    def coulomb_term():
        factored = jnp.dot(coulomb_factors, full, preferred_element_type=jnp.float32).astype(
            jnp.bfloat16
        )
        return 2.0 * lax.dot_general(
            coulomb_factors, factored, (((0,), (0,)), ((), ())), preferred_element_type=jnp.float32
        )

    def grid_term(first, last):

        def step(carry, items):
            occ, vir, weight, live = items
            trans = jnp.dot(vir, rearranged, preferred_element_type=jnp.float32).reshape(
                batch_size, occ_count, width
            )
            occ_float = occ.astype(jnp.float32)
            density = jnp.einsum("gik,ig->gk", trans, occ_float)
            mask = (slots < live).astype(jnp.float32)
            weighted = density * (weight * mask)[:, None]
            scaled = (
                (occ_float.T[:, :, None] * weighted[:, None, :])
                .reshape(batch_size, occ_count * width)
                .astype(jnp.bfloat16)
            )
            return (
                carry
                + lax.dot_general(
                    vir, scaled, (((0,), (0,)), ((), ())), preferred_element_type=jnp.float32
                ),
                None,
            )

        start = jnp.zeros((vir_count, occ_count * width), jnp.float32)
        items = (
            occ_values[first:last],
            vir_values[first:last],
            kernel[first:last],
            live_points[first:last],
        )
        total, _ = lax.scan(step, start, items)
        return (
            total.reshape(vir_count, occ_count, width)
            .transpose(1, 0, 2)
            .reshape(occ_count * vir_count, width)
        )

    cut = batches // 2

    def first_group():
        return coulomb_term() + grid_term(0, cut)

    def second_group():
        return grid_term(cut, batches)

    partial_sum = lax.cond(lax.axis_index("grp") == 0, first_group, second_group)
    summed = lax.psum_scatter(partial_sum, ("grp", "blk"), scatter_dimension=0, tiled=True)
    joined = lax.all_to_all(summed, "vec", split_axis=0, concat_axis=1, tiled=True)
    result = energy_gap[:, None] * trial.astype(jnp.float32) + joined
    return result.astype(jnp.bfloat16)


def solution(mesh):
    in_specs = (
        P(("grp", "blk", "vec"), None),
        P(("grp", "blk", "vec")),
        P("blk", None),
        P("blk", None, None),
        P("blk", None, None),
        P("blk", None),
        P("blk"),
    )
    out_specs = P(("grp", "blk", "vec"), None)
    return jax.shard_map(local, mesh=mesh, in_specs=in_specs, out_specs=out_specs, check_vma=False)
```

profile of v0, /device:TPU:0, one launch (start us, length us, event | category | flops | bytes accessed | tf_op | source)
XLA Modules:
  0.0 206.8 jit_solution(335047641834568448)
XLA Ops:
  6.5 3.3 %all-to-all-start = ((bf16[640,2,16]{0,2,1:T(8,128)(2,1)}), bf16[640,2,16]{0,2,1:T(8,128)(2,1)S(1)}, u32[]{:S(2)}, u32[]{:S(2)}) async-start(bf16[640,2,16]{0,2,1:T(8,128)(2,1)} %bitcast.130), calls=%async_computation | async-start | bytes 81920 | tf_op jit(solution)/shard_map/all_to_all | solution.py:8
  9.9 1.3 all-to-all-done
  11.2 46.4 %all_gather.3 = bf16[20480,16]{0,1:T(8,128)(2,1)S(1)} all-gather(bf16[1280,16]{0,1:T(8,128)(2,1)S(1)} %bitcast.131), channel_id=1, replica_groups=mesh['grp'=2,'blk'=8,'vec'=2] {'grp','blk'}, dimensions={0}, use_global_device_ids=true | all-gather | bytes 696320 | tf_op jit(solution)/shard_map/all_gather | solution.py:9
  58.0 0.6 copy-done.1
  58.6 60.6 %conditional.1 = (f32[20480,16]{0,1:T(8,128)}) conditional(s32[]{:T(128)} %convert_element_type.41, (bf16[10,40,512]{2,1,0:T(8,128)(2,1)S(1)}, bf16[10,512,512]{2,1,0:T(8,128)(2,1)}, f32[10,512]{1,0:T(8,128)S(1)}, s32[10]{0:T(128)S(1)}, bf16[512,640]{0,1:T(8,128)(2,1)S(1)}, /*index=5*/s32[512]{0:T(512)S(1)}) %tuple.68, (bf16[512,20480]{1,0:T(8,128)(2,1)}, ...), branch_computations={%region_0.3_spmd, %region_3.6_spmd} | conditional | flops 1344848896 | bytes 43934980 | solution.py:76
  58.6 3.8 %slice.20 = bf16[5,512,512]{2,1,0:T(8,128)(2,1)} slice(bf16[10,512,512]{2,1,0:T(8,128)(2,1)} %get-tuple-element.127), slice={[0:5], [0:512], [0:512]} | slice | bytes 5242880 | tf_op jit(solution)/shard_map/cond/branch_1_fun/slice | solution.py:57
  62.4 28.0 %while.21 = (s32[]{:T(128)}, f32[512,640]{1,0:T(8,128)S(1)}, bf16[5,512,512]{2,1,0:T(8,128)(2,1)}, bf16[5,40,512]{2,1,0:T(8,128)(2,1)S(1)}, bf16[512,640]{0,1:T(...) while((s32[]{:T(128)}, f32[512,640]{1,0:T(8,128)S(1)}, ...), condition=%wide.region_5.5_spmd.clone, body=%wide.region_4.4_spmd.clone.sunk | while | flops 673096704 | bytes 6149255 | solution.py:61
  62.4 2.0 fusion.38
  64.4 0.7 dynamic_slice.72
  65.1 0.7 compare_select_fusion.4
  65.9 2.1 convolution_add_fusion.4
  68.0 2.0 fusion.38
  70.0 0.7 dynamic_slice.72
  70.7 0.7 compare_select_fusion.4
  71.5 2.1 convolution_add_fusion.4
  73.6 2.0 fusion.38
  75.6 0.7 dynamic_slice.72
  76.3 0.7 compare_select_fusion.4
  77.1 2.1 convolution_add_fusion.4
  79.2 2.0 fusion.38
  81.2 0.7 dynamic_slice.72
  81.9 0.7 compare_select_fusion.4
  82.7 2.1 convolution_add_fusion.4
  84.8 2.0 fusion.38
  86.8 0.7 dynamic_slice.72
  87.5 0.7 compare_select_fusion.4
  88.3 2.1 convolution_add_fusion.4
  90.9 28.3 %fusion.17 = f32[20480,16]{0,1:T(8,128)} fusion(f32[20480,16]{0,1:T(8,128)S(1)} %bitcast.118, bf16[512,20480]{1,0:T(8,128)(2,1)} %get-tuple-element.135, bf16[20480,16]{0,1:T(8,128)(2,1)S(1)} %get-tuple-element.126), kind=kOutput, calls=%fused_computation.34 | convolution fusion | flops 671752192 | bytes 24248320 | tf_op jit(solution)/shard_map/cond/branch_1_fun/dot_general | solution.py:26
  119.2 75.5 %reduce-scatter.2.cloned.1.call-done = f32[1280,16]{0,1:T(8,128)} async-done(((f32[20480,16]{0,1:T(8,128)}), f32[1280,16]{0,1:T(8,128)}) %reduce-scatter.2.cloned.1.call-update) | async-done | bytes 81936 | tf_op jit(solution)/shard_map/reduce_scatter | solution.py:77
  194.7 0.9 copy.71
  195.6 3.8 %all_to_all.38 = f32[2,640,16]{1,2,0:T(8,128)S(1)} all-to-all(f32[2,640,16]{1,2,0:T(8,128)S(1)} %bitcast.126), channel_id=1, replica_groups=mesh['grp'=2,'blk'=8,'vec'=2] {'vec'}, dimensions={0} | all-to-all | bytes 163840 | tf_op jit(solution)/shard_map/all_to_all | solution.py:78
  199.3 0.6 fusion.18
  (43 shorter events, 1.7 us)
Async XLA Ops:
  6.5 4.7 %all-to-all-start = ((bf16[640,2,16]{0,2,1:T(8,128)(2,1)}), bf16[640,2,16]{0,2,1:T(8,128)(2,1)S(1)}, u32[]{:S(2)}, u32[]{:S(2)}) async-start(bf16[640,2,16]{0,2,1:T(8,128)(2,1)} %bitcast.130), calls=%async_computation | async-start | bytes 81920 | tf_op jit(solution)/shard_map/all_to_all | solution.py:8
  9.8 184.9 %reduce-scatter.2.cloned.1.call-start = ((), (), s32[]{:S(2)}) async-start(), calls=%async_computation.3 | async-start | bytes 1392640 | tf_op jit(solution)/shard_map/reduce_scatter | solution.py:77
  57.6 1.0 copy-start.1
  57.6 1.0 copy-start.3
  57.6 1.0 copy-start.5
  58.6 3.8 %copy-start = (bf16[512,640]{0,1:T(8,128)(2,1)}, bf16[512,640]{0,1:T(8,128)(2,1)S(1)}, u32[]{:S(2)}) copy-start(bf16[512,640]{0,1:T(8,128)(2,1)S(1)} %get-tuple-element.336) | copy-start | bytes 1966084 | tf_op jit(solution)/shard_map/cond
  119.2 80.1 %copy-start.2 = (bf16[640,32]{0,1:T(8,128)(2,1)S(1)}, bf16[640,32]{0,1:T(8,128)(2,1)}, u32[]{:S(2)}) copy-start(bf16[640,32]{0,1:T(8,128)(2,1)} %param.13) | copy-start | bytes 122884
  119.2 80.1 %copy-start.4 = (f32[640]{0:T(1024)S(1)}, f32[640]{0:T(1024)}, u32[]{:S(2)}) copy-start(f32[640]{0:T(1024)} %param.14) | copy-start | bytes 7684
Sparse Core Ops, SparseCore 0:
  119.3 75.2 reduce-scatter.1
where the time goes:
time: 208 us; the launch traced here: 207 us
  waiting for transfers between devices  76.8 us (37%)
  blocking collectives  50.1 us (24%)
  matrix products  48.4 us (23%)
  between operations  13.4 us (6%)
  local copies, waits for them, and re-layouts  9.57 us (5%)
  other arithmetic  4.78 us (2%)
  starting transfers between devices  3.31 us (2%)
    reduce_scatter x1, waiting for transfers between devices, local(): lax.psum_scatter(partial_sum, ('grp', 'blk'), scatter_dimension=0, tiled=...  75.5 us
    all_gather x1, blocking collectives, local(): full = lax.all_gather(pair_rows, ('grp', 'blk'), axis=0, tiled=True)  46.4 us
    dot_general x1, matrix products, coulomb_term(): lax.dot_general(coulomb_factors, factored, (((0,), (0,)), ((), ())), pref...  28.3 us
    dot_general x5, matrix products, step(): lax.dot_general(vir, scaled, (((0,), (0,)), ((), ())), preferred_element_...  10.3 us
    dot_general x5, matrix products, step(): jnp.dot(vir, rearranged, preferred_element_type=jnp.float32)  9.84 us
  transfers between devices with their start and end apart: 2, of which 2 were waited for; matrix products, arithmetic and copies ran while one was open for 0% of the time, Pallas kernels for 0%

commit v1 on v0

--- a/solution.py
+++ b/solution.py
@@ -1,10 +1,19 @@
+import functools
+
 import jax
 import jax.numpy as jnp
 from jax import lax
+from jax.experimental import pallas as pl
+from jax.experimental.pallas import tpu as pltpu
 from jax.sharding import PartitionSpec as P
 
-
-def local(trial, energy_gap, coulomb_factors, occ_values, vir_values, kernel, live_points):
+LANES = 128
+MESH = pl.DeviceIdType.MESH
+
+
+def collective_local(
+    trial, energy_gap, coulomb_factors, occ_values, vir_values, kernel, live_points
+):
     pair_rows = lax.all_to_all(trial, "vec", split_axis=1, concat_axis=0, tiled=True)
     full = lax.all_gather(pair_rows, ("grp", "blk"), axis=0, tiled=True)
     occ_count = occ_values.shape[1]
@@ -80,6 +89,373 @@
     return result.astype(jnp.bfloat16)
 
 
+def fused_kernel(
+    nz,
+    trial_ref,
+    gap_ref,
+    cf_hbm,
+    occ_hbm,
+    vir_hbm,
+    weight_ref,
+    live_ref,
+    out_ref,
+    full,
+    rear,
+    cf,
+    occ,
+    vir,
+    scaled,
+    exchange,
+    partial,
+    land_d,
+    send_a,
+    land_a,
+    send_b,
+    land_b,
+    send_z,
+    land_z,
+    local_sem,
+    load_sem,
+    gs_send,
+    gs_recv,
+    gd_send,
+    gd_recv,
+    rs_send,
+    rs_recv,
+    rd_send,
+    rd_recv,
+):
+    f32, bf16 = jnp.float32, jnp.bfloat16
+    blocks, _, chunks, width, _ = full.shape
+    g, b, v = lax.axis_index("grp"), lax.axis_index("blk"), lax.axis_index("vec")
+    z, y = b // 2, lax.rem(b, 2)
+    g1, y1 = g + v * (1 - 2 * g), y + (1 - v) * (1 - 2 * y)
+    g2, y2 = g + (1 - v) * (1 - 2 * g), y + v * (1 - 2 * y)
+    g3, y3 = 1 - g, 1 - y
+    quarter = g * 2 + v
+    batches, occ_count, part = occ.shape
+    vir_count = vir.shape[2]
+    cf_rows = cf.shape[0]
+    per_occ = vir_count // LANES
+
+    def zed(n):
+        return lax.rem(z + nz - n, nz)
+
+    def block(gg, n, yy):
+        return gg * (2 * nz) + zed(n) * 2 + yy
+
+    def at(gg, zz, yy, vv):
+        return (gg, zz * 2 + yy, vv)
+
+    p1, p2, twin = at(g1, z, y1, v), at(g2, z, y2, v), at(g, z, y, 1 - v)
+
+    barrier = pltpu.get_barrier_semaphore()
+    peers = [p1, p2, twin] + [at(g, zed(n), y, v) for n in range(1, nz)]
+    for peer in peers:
+        pl.semaphore_signal(barrier, inc=1, device_id=peer, device_id_type=MESH)
+
+    own = block(g, 0, y)
+    local = [
+        pltpu.make_async_copy(
+            trial_ref.at[:, pl.ds(c * LANES, LANES)], full.at[own, v, c], local_sem.at[c]
+        )
+        for c in range(chunks)
+    ]
+    for copy in local:
+        copy.start()
+    first_slot = pl.multiple_of(quarter * part, part)
+    loads = [
+        pltpu.make_async_copy(
+            vir_hbm.at[:, pl.ds(first_slot, part), :], vir, load_sem.at[0]
+        ),
+        pltpu.make_async_copy(
+            occ_hbm.at[:, :, pl.ds(first_slot, part)], occ, load_sem.at[1]
+        ),
+        pltpu.make_async_copy(
+            cf_hbm.at[pl.ds(pl.multiple_of(quarter * cf_rows, cf_rows), cf_rows), :],
+            cf,
+            load_sem.at[2],
+        ),
+    ]
+    for copy in local:
+        copy.wait()
+    pl.semaphore_wait(barrier, len(peers))
+
+    near = sorted(range(1, nz), key=lambda n: min(n, nz - n))
+    sent = []
+
+    def gather(index, sender_block, vv, peer, send, recv):
+        return pltpu.make_async_remote_copy(
+            src_ref=full.at[sender_block, vv],
+            dst_ref=full.at[sender_block, vv],
+            send_sem=send.at[index],
+            recv_sem=recv.at[index],
+            device_id=peer,
+            device_id_type=MESH,
+        )
+
+    def push(index, blk_index, peer):
+        copy = gather(index, blk_index, v, peer, gs_send, gs_recv)
+        copy.start()
+        sent.append(copy)
+
+    def push_twin(index, blk_index):
+        copy = gather(index, blk_index, v, twin, gd_send, gd_recv)
+        copy.start()
+        sent.append(copy)
+
+    def arrive(index, blk_index):
+        gather(index, blk_index, v, p1, gs_send, gs_recv).wait_recv()
+
+    base1, base2 = nz, 2 * nz
+    for n in near[::-1]:
+        push(n, own, at(g, lax.rem(z + n, nz), y, v))
+    push(base1, own, p1)
+    push(base2, own, p2)
+    push_twin(0, own)
+    for copy in loads:
+        copy.start()
+    for n in near:
+        j = block(g, n, y)
+        arrive(n, j)
+        push(base1 + n, j, p1)
+        push(base2 + n, j, p2)
+        push_twin(n, j)
+    for n in [0] + near:
+        j = block(g1, n, y1)
+        arrive(base1 + n, j)
+        push(base2 + nz + n, j, p2)
+        push_twin(nz + n, j)
+    for half, (gg, yy) in enumerate(((g2, y2), (g3, y3))):
+        for n in [0] + near:
+            j = block(gg, n, yy)
+            arrive(base2 + half * nz + n, j)
+            push_twin((2 + half) * nz + n, j)
+    for kind, (gg, yy) in enumerate(((g, y), (g2, y2), (g1, y1), (g3, y3))):
+        for n in [0] + near:
+            gather(kind * nz + n, block(gg, n, yy), 1 - v, twin, gd_send, gd_recv).wait_recv()
+    for copy in sent:
+        copy.wait_send()
+    for copy in loads:
+        copy.wait()
+
+    for i in range(occ_count):
+        for c in range(per_occ):
+            chunk = i * per_occ + c
+            rear[pl.ds(i * width, width), pl.ds(c * LANES, LANES)] = full[
+                chunk // (2 * chunks), (chunk // chunks) % 2, chunk % chunks
+            ]
+
+    weights = weight_ref[:, pl.ds(first_slot, part)]
+    line = lax.broadcasted_iota(jnp.int32, weights.shape, 0)
+    slot = first_slot + lax.broadcasted_iota(jnp.int32, (1, part), 1)
+
+    def grid_step(t, _):
+        v_t = vir[t]
+        trans = lax.dot_general(
+            rear[...], v_t, (((1,), (1,)), ((), ())), preferred_element_type=f32
+        )
+        o = occ[t].astype(f32)
+        density = jnp.sum(trans.reshape(occ_count, width, part) * o[:, None, :], axis=0)
+        weight = jnp.sum(jnp.where(line == t, weights, 0.0), axis=0, keepdims=True)
+        weight = jnp.where(slot < live_ref[t], weight, 0.0)
+        weighted = density * weight
+        values = (o[:, None, :] * weighted[None, :, :]).reshape(occ_count * width, part)
+        scaled[t] = values.astype(bf16)
+        return 0
+
+    lax.fori_loop(0, batches, grid_step, 0)
+
+    def factor_step(i, total):
+        rows = rear[pl.ds(pl.multiple_of(i * width, width), width), :]
+        cols = cf[:, pl.ds(pl.multiple_of(i * vir_count, vir_count), vir_count)]
+        return total + lax.dot_general(
+            rows, cols, (((1,), (1,)), ((), ())), preferred_element_type=f32
+        )
+
+    factored = lax.fori_loop(
+        0, occ_count, factor_step, jnp.zeros((width, cf_rows), f32), unroll=4
+    )
+    doubled = (2.0 * factored.astype(bf16).astype(f32)).astype(bf16)
+
+    group = 5
+    rows = (occ_count // group) * width
+
+    def exchange_step(r, _):
+        lines = pl.ds(pl.multiple_of(r * rows, rows), rows)
+        s = jnp.concatenate([scaled[t, lines, :] for t in range(batches)], axis=1)
+        exchange[lines, :] = jnp.dot(
+            s, vir[...].reshape(batches * part, vir_count), preferred_element_type=f32
+        )
+        return 0
+
+    lax.fori_loop(0, group, exchange_step, 0)
+
+    for i in range(occ_count):
+        lines = exchange[pl.ds(i * width, width), :] + jnp.dot(
+            doubled, cf[:, pl.ds(i * vir_count, vir_count)], preferred_element_type=f32
+        )
+        for c in range(per_occ):
+            chunk = i * per_occ + c
+            partial[chunk // (2 * chunks), (chunk // chunks) % 2, chunk % chunks] = lines[
+                :, c * LANES : (c + 1) * LANES
+            ]
+
+    far = near[::-1] + [0]
+    drain = []
+
+    def twin_copy(index, j, vv):
+        return pltpu.make_async_remote_copy(
+            src_ref=partial.at[j, vv],
+            dst_ref=land_d.at[j],
+            send_sem=rd_send.at[index],
+            recv_sem=rd_recv.at[index],
+            device_id=twin,
+            device_id_type=MESH,
+        )
+
+    for kind, (gg, yy) in enumerate(((g3, y3), (g1, y1), (g2, y2), (g, y))):
+        for n in far:
+            copy = twin_copy(kind * nz + n, block(gg, n, yy), 1 - v)
+            copy.start()
+            drain.append(copy)
+
+    def wire(src, dst, slot_index, index, peer):
+        return pltpu.make_async_remote_copy(
+            src_ref=src.at[slot_index],
+            dst_ref=dst.at[slot_index],
+            send_sem=rs_send.at[index],
+            recv_sem=rs_recv.at[index],
+            device_id=peer,
+            device_id_type=MESH,
+        )
+
+    def pair_sum(kind, n, j):
+        twin_copy(kind * nz + n, j, 1 - v).wait_recv()
+        return partial[j, v] + land_d[j]
+
+    for kind, (gg, yy) in enumerate(((g3, y3), (g2, y2))):
+        for n in far:
+            k = kind * nz + n
+            send_a[k] = pair_sum(kind, n, block(gg, n, yy)).astype(bf16)
+            copy = wire(send_a, land_a, k, k, p2)
+            copy.start()
+            drain.append(copy)
+    for n in far:
+        total = pair_sum(2, n, block(g1, n, y1))
+        wire(send_a, land_a, n, n, p2).wait_recv()
+        send_b[n] = (total + land_a[n].astype(f32)).astype(bf16)
+        copy = wire(send_b, land_b, n, 2 * nz + n, p1)
+        copy.start()
+        drain.append(copy)
+    for n in far:
+        total = pair_sum(3, n, block(g, n, y))
+        wire(send_a, land_a, nz + n, nz + n, p2).wait_recv()
+        total = total + land_a[nz + n].astype(f32)
+        wire(send_b, land_b, n, 2 * nz + n, p1).wait_recv()
+        total = total + land_b[n].astype(f32)
+        if n > 0:
+            send_z[n - 1] = total.astype(bf16)
+            copy = wire(send_z, land_z, n - 1, 3 * nz + n, at(g, zed(n), y, v))
+            copy.start()
+            drain.append(copy)
+    for n in near:
+        wire(send_z, land_z, n - 1, 3 * nz + n, p1).wait_recv()
+        total = total + land_z[n - 1].astype(f32)
+    for c in range(chunks):
+        lanes = pl.ds(c * LANES, LANES)
+        mine = full[own, v, c].astype(f32)
+        out_ref[:, lanes] = (gap_ref[:, lanes] * mine + total[c]).astype(bf16)
+    for copy in drain:
+        copy.wait_send()
+
+
+def fused_local(
+    blk, trial, energy_gap, coulomb_factors, occ_values, vir_values, kernel, live_points
+):
+    pairs, width = trial.shape
+    blocks = 2 * blk
+    nz = blk // 2
+    chunks = pairs // LANES
+    batches, occ_count, batch_size = occ_values.shape
+    vir_count = vir_values.shape[2]
+    part = batch_size // 4
+    cf_rows = coulomb_factors.shape[0] // 4
+    bf16, f32 = jnp.bfloat16, jnp.float32
+    vmem = pl.BlockSpec(memory_space=pltpu.VMEM)
+    anywhere = pl.BlockSpec(memory_space=pl.ANY)
+    dma = pltpu.SemaphoreType.DMA
+    out = pl.pallas_call(
+        functools.partial(fused_kernel, nz),
+        out_shape=jax.ShapeDtypeStruct((width, pairs), bf16),
+        in_specs=[
+            anywhere,
+            vmem,
+            anywhere,
+            anywhere,
+            anywhere,
+            vmem,
+            pl.BlockSpec(memory_space=pltpu.SMEM),
+        ],
+        out_specs=vmem,
+        scratch_shapes=[
+            pltpu.VMEM((blocks, 2, chunks, width, LANES), bf16),
+            pltpu.VMEM((occ_count * width, vir_count), bf16),
+            pltpu.VMEM((cf_rows, coulomb_factors.shape[1]), bf16),
+            pltpu.VMEM((batches, occ_count, part), bf16),
+            pltpu.VMEM((batches, part, vir_count), bf16),
+            pltpu.VMEM((batches, occ_count * width, part), bf16),
+            pltpu.VMEM((occ_count * width, vir_count), f32),
+            pltpu.VMEM((blocks, 2, chunks, width, LANES), f32),
+            pltpu.VMEM((blocks, chunks, width, LANES), f32),
+            pltpu.VMEM((2 * nz, chunks, width, LANES), bf16),
+            pltpu.VMEM((2 * nz, chunks, width, LANES), bf16),
+            pltpu.VMEM((nz, chunks, width, LANES), bf16),
+            pltpu.VMEM((nz, chunks, width, LANES), bf16),
+            pltpu.VMEM((nz, chunks, width, LANES), bf16),
+            pltpu.VMEM((nz, chunks, width, LANES), bf16),
+            dma((chunks,)),
+            dma((3,)),
+            dma((4 * nz,)),
+            dma((4 * nz,)),
+            dma((4 * nz,)),
+            dma((4 * nz,)),
+            dma((4 * nz,)),
+            dma((4 * nz,)),
+            dma((4 * nz,)),
+            dma((4 * nz,)),
+        ],
+        compiler_params=pltpu.CompilerParams(
+            collective_id=0, has_side_effects=True, vmem_limit_bytes=56 * 1024 * 1024
+        ),
+    )(
+        trial.T,
+        energy_gap[None, :],
+        coulomb_factors,
+        occ_values,
+        vir_values,
+        kernel,
+        live_points,
+    )
+    return out.T
+
+
+def fits(mesh):
+    def check(trial, coulomb_factors, occ_values, vir_values):
+        return (
+            mesh.shape["grp"] == 2
+            and mesh.shape["vec"] == 2
+            and mesh.shape["blk"] % 4 == 0
+            and trial.shape[0] % LANES == 0
+            and coulomb_factors.shape[0] % (4 * LANES) == 0
+            and occ_values.shape[2] % (4 * LANES) == 0
+            and occ_values.shape[1] % 5 == 0
+            and vir_values.shape[2] % LANES == 0
+        )
+
+    return check
+
+
 def solution(mesh):
     in_specs = (
         P(("grp", "blk", "vec"), None),
@@ -91,4 +467,12 @@
         P("blk"),
     )
     out_specs = P(("grp", "blk", "vec"), None)
+    check = fits(mesh)
+
+    def local(trial, energy_gap, coulomb_factors, occ_values, vir_values, kernel, live_points):
+        args = (trial, energy_gap, coulomb_factors, occ_values, vir_values, kernel, live_points)
+        if check(trial, coulomb_factors, occ_values, vir_values):
+            return fused_local(mesh.shape["blk"], *args)
+        return collective_local(*args)
+
     return jax.shard_map(local, mesh=mesh, in_specs=in_specs, out_specs=out_specs, check_vma=False)

time: 208 us -> 47.8 us (0.23)
  waiting for transfers between devices: 76.8 us -> 0 us
  blocking collectives: 50.1 us -> 0 us
  matrix products: 48.4 us -> 0 us
  Pallas kernels: 0 us -> 44.8 us
  between operations: 13.4 us -> 0.01 us
  local copies, waits for them, and re-layouts: 9.57 us -> 2.67 us
  other arithmetic: 4.78 us -> 0 us
  starting transfers between devices: 3.31 us -> 0 us
    reduce_scatter x1 -> x0, waiting for transfers between devices: 75.5 us -> none  [local(): lax.psum_scatter(partial_sum, ('grp', 'blk'), scatter_dimension=0, tiled=...]
    dot_general x11 -> x0, matrix products: 48.4 us -> none  [the longest x1 28.3 us: coulomb_term(): lax.dot_general(coulomb_factors, factored, (((0,), (0,)), ((), ())), pref...]
    all_gather x1 -> x0, blocking collectives: 46.4 us -> none  [local(): full = lax.all_gather(pair_rows, ('grp', 'blk'), axis=0, tiled=True)]
    pallas_call x0 -> x1, Pallas kernels: none -> 44.8 us  [fused_local(): pl.pallas_call(functools.partial(fused_kernel, nz), out_shape=jax.ShapeDt...]
    slice x3 -> x0, local copies, waits for them, and re-layouts: 3.78 us -> none  [the longest x1 3.76 us: grid_term(): vir_values[first:last]]
    all_to_all x1 -> x0, blocking collectives: 3.76 us -> none  [local(): lax.all_to_all(summed, 'vec', split_axis=0, concat_axis=1, tiled=True)]
    mul x10 -> x0, other arithmetic: 3.49 us -> none  [step(): weighted = density * (weight * mask)[:, None]]
    dynamic_slice x10 -> x0, local copies, waits for them, and re-layouts: 3.41 us -> none  [grid_term(): total, _ = lax.scan(step, start, items)]
  transfers between devices with their start and end apart: 2 -> 0, of which waited for: 2 -> 0; matrix products, arithmetic and copies ran while one was open for 0% -> 0% of each run, Pallas kernels for 0% -> 0%
where the time goes in v1:
time: 47.8 us; the launch traced here: 47.4 us
  Pallas kernels  44.8 us (94%)
  local copies, waits for them, and re-layouts  2.67 us (6%)
    pallas_call x1, Pallas kernels, fused_local(): pl.pallas_call(functools.partial(fused_kernel, nz), out_shape=jax.ShapeDt...  44.8 us
    unnamed x1, local copies, waits for them, and re-layouts  1.4 us
    broadcast_in_dim x1, local copies, waits for them, and re-layouts, fused_local(): energy_gap[None, :]  1.27 us

profile of v1, /device:TPU:0, one launch (start us, length us, event | category | flops | bytes accessed | tf_op | source)
XLA Modules:
  0.0 47.4 jit_solution(7076782610759500192)
XLA Ops:
  0.0 1.3 %broadcast_in_dim.3.gap_ref = f32[1,640]{1,0:T(1,128)} reshape(f32[640]{0:T(1024)} %param.8) | data formatting | bytes 5120 | tf_op jit(solution)/shard_map/broadcast_in_dim | solution.py:433
  1.3 44.8 %shard_map.73 = bf16[32,640]{1,0:T(8,128)(2,1)} custom-call(bf16[32,640]{1,0:T(8,128)(2,1)} %bitcast.3, f32[1,640]{1,0:T(1,128)} %broadcast_in_dim.3.gap_ref, bf16[512,20480]{1,0:T(8,128)(2,1)} %cf_hbm.1, bf16[10,40,512]{2,1,0:T(8,128)(2,1)} %occ_hbm.1, bf16[10,512,512]{2,1,0:T(8,128)(2,1)} %vir_hbm.1, f32[10,512]{1,0:T(8,128)} %weight_ref.1, s32[10]{0:T(128)} %live_ref.1), custom_call_target="tpu_custom_call" | custom-call | tf_op jit(solution)/shard_map/pallas_call | solution.py:388
  46.0 1.4 %copy.9 = bf16[640,32]{0,1:T(8,128)(2,1)} copy(bf16[640,32]{0,1:T(8,128)(2,1)} %bitcast.2) | data formatting | bytes 81920

commit v2 on v1

v2 whole, which is shorter than its diff:
```python
import functools

import jax
import jax.numpy as jnp
from jax import lax
from jax.experimental import pallas as pl
from jax.experimental.pallas import tpu as pltpu
from jax.sharding import PartitionSpec as P

LANES = 128
MESH = pl.DeviceIdType.MESH


def collective_local(
    trial, energy_gap, coulomb_factors, occ_values, vir_values, kernel, live_points
):
    pair_rows = lax.all_to_all(trial, "vec", split_axis=1, concat_axis=0, tiled=True)
    full = lax.all_gather(pair_rows, ("grp", "blk"), axis=0, tiled=True)
    occ_count = occ_values.shape[1]
    batch_size = occ_values.shape[2]
    vir_count = vir_values.shape[2]
    width = full.shape[1]
    batches = occ_values.shape[0]
    rearranged = (
        full.reshape(occ_count, vir_count, width)
        .transpose(1, 0, 2)
        .reshape(vir_count, occ_count * width)
    )
    slots = jnp.arange(batch_size, dtype=jnp.int32)

    def coulomb_term():
        factored = jnp.dot(coulomb_factors, full, preferred_element_type=jnp.float32).astype(
            jnp.bfloat16
        )
        return 2.0 * lax.dot_general(
            coulomb_factors, factored, (((0,), (0,)), ((), ())), preferred_element_type=jnp.float32
        )

    def grid_term(first, last):

        def step(carry, items):
            occ, vir, weight, live = items
            trans = jnp.dot(vir, rearranged, preferred_element_type=jnp.float32).reshape(
                batch_size, occ_count, width
            )
            occ_float = occ.astype(jnp.float32)
            density = jnp.einsum("gik,ig->gk", trans, occ_float)
            mask = (slots < live).astype(jnp.float32)
            weighted = density * (weight * mask)[:, None]
            scaled = (
                (occ_float.T[:, :, None] * weighted[:, None, :])
                .reshape(batch_size, occ_count * width)
                .astype(jnp.bfloat16)
            )
            return (
                carry
                + lax.dot_general(
                    vir, scaled, (((0,), (0,)), ((), ())), preferred_element_type=jnp.float32
                ),
                None,
            )

        start = jnp.zeros((vir_count, occ_count * width), jnp.float32)
        items = (
            occ_values[first:last],
            vir_values[first:last],
            kernel[first:last],
            live_points[first:last],
        )
        total, _ = lax.scan(step, start, items)
        return (
            total.reshape(vir_count, occ_count, width)
            .transpose(1, 0, 2)
            .reshape(occ_count * vir_count, width)
        )

    cut = batches // 2

    def first_group():
        return coulomb_term() + grid_term(0, cut)

    def second_group():
        return grid_term(cut, batches)

    partial_sum = lax.cond(lax.axis_index("grp") == 0, first_group, second_group)
    summed = lax.psum_scatter(partial_sum, ("grp", "blk"), scatter_dimension=0, tiled=True)
    joined = lax.all_to_all(summed, "vec", split_axis=0, concat_axis=1, tiled=True)
    result = energy_gap[:, None] * trial.astype(jnp.float32) + joined
    return result.astype(jnp.bfloat16)


def fused_kernel(
    nz,
    trial_ref,
    cf_hbm,
    occ_hbm,
    vir_hbm,
    weight_ref,
    live_ref,
    out_ref,
    full,
    rear,
    cf,
    occ,
    occ_float,
    vir,
    density,
    factored,
    partial,
    land_d,
    send_a,
    land_a,
    send_b,
    land_b,
    send_z,
    land_z,
    local_sem,
    load_sem,
    gs_send,
    gs_recv,
    gd_send,
    gd_recv,
    rs_send,
    rs_recv,
    rd_send,
    rd_recv,
):
    f32, bf16 = jnp.float32, jnp.bfloat16
    _, _, chunks, width, _ = full.shape
    g, b, v = lax.axis_index("grp"), lax.axis_index("blk"), lax.axis_index("vec")
    z, y = b // 2, lax.rem(b, 2)
    g1, y1 = g + v * (1 - 2 * g), y + (1 - v) * (1 - 2 * y)
    g2, y2 = g + (1 - v) * (1 - 2 * g), y + v * (1 - 2 * y)
    g3, y3 = 1 - g, 1 - y
    kind1, kind2 = 1 + v, 2 - v
    quarter = g * 2 + v
    batches, occ_count, part = occ.shape
    vir_count = vir.shape[2]
    points = batches * part
    cf_rows = cf.shape[0]
    per_occ = vir_count // LANES
    group_occ = 4 * chunks // per_occ
    lines = group_occ * width
    step = 2 if batches % 2 == 0 else 1

    def zed(n):
        return lax.rem(z + nz - n, nz)

    def block(gg, n, yy):
        return gg * (2 * nz) + zed(n) * 2 + yy

    def at(gg, zz, yy, vv):
        return (gg, zz * 2 + yy, vv)

    p1, p2, twin = at(g1, z, y1, v), at(g2, z, y2, v), at(g, z, y, 1 - v)

    barrier = pltpu.get_barrier_semaphore()
    peers = [p1, p2, twin] + [at(g, zed(n), y, v) for n in range(1, nz)]
    for peer in peers:
        pl.semaphore_signal(barrier, inc=1, device_id=peer, device_id_type=MESH)

    own = block(g, 0, y)
    local = [
        pltpu.make_async_copy(
            trial_ref.at[:, pl.ds(c * LANES, LANES)], full.at[own, v, c], local_sem.at[c]
        )
        for c in range(chunks)
    ]
    for copy in local:
        copy.start()
    first_slot = pl.multiple_of(quarter * part, part)
    loads = [
        pltpu.make_async_copy(
            occ_hbm.at[:, :, pl.ds(first_slot, part)], occ, load_sem.at[0]
        ),
        pltpu.make_async_copy(
            vir_hbm.at[:, pl.ds(first_slot, part), :], vir, load_sem.at[1]
        ),
        pltpu.make_async_copy(
            cf_hbm.at[pl.ds(pl.multiple_of(quarter * cf_rows, cf_rows), cf_rows), :],
            cf,
            load_sem.at[2],
        ),
    ]
    for copy in loads:
        copy.start()
    for copy in local:
        copy.wait()
    pl.semaphore_wait(barrier, len(peers))

    near = sorted(range(1, nz), key=lambda n: min(n, nz - n))
    order = [0] + near
    sent = []

    def gather(index, j, vv, peer, send, recv):
        return pltpu.make_async_remote_copy(
            src_ref=full.at[j, vv],
            dst_ref=full.at[j, vv],
            send_sem=send.at[index],
            recv_sem=recv.at[index],
            device_id=peer,
            device_id_type=MESH,
        )

    def push(index, j, peer):
        copy = gather(index, j, v, peer, gs_send, gs_recv)
        copy.start()
        sent.append(copy)

    def push_twin(kind, n, j):
        copy = gather(kind * nz + n, j, v, twin, gd_send, gd_recv)
        copy.start()
        sent.append(copy)

    def arrive(index, j):
        gather(index, j, v, p1, gs_send, gs_recv).wait_recv()

    def from_twin(kind, n, j):
        gather(kind * nz + n, j, 1 - v, twin, gd_send, gd_recv).wait_recv()

    def absorb(gg, fx, n, slot):
        from_twin(2 * fx, n, block(gg, n, y))
        from_twin(2 * fx + 1, n, block(gg, n, y3))
        group = gg * nz + zed(n)
        for m in range(4 * chunks):
            i, c = m // per_occ, m % per_occ
            rear[slot, i * width : (i + 1) * width, c * LANES : (c + 1) * LANES] = full[
                group * 2 + m // (2 * chunks), (m // chunks) % 2, m % chunks
            ]
        for t in range(0, batches, step):
            span = slice(t * part, (t + step) * part)
            trans = lax.dot_general(
                rear[slot],
                vir[t : t + step].reshape(step * part, vir_count),
                (((1,), (1,)), ((), ())),
                preferred_element_type=f32,
            )
            o = occ_float[group, :, span]
            term = jnp.sum(trans.reshape(group_occ, width, step * part) * o[:, None, :], axis=0)
            density[:, span] = term if slot == 0 else density[:, span] + term
        total = None
        for i in range(group_occ):
            start = pl.multiple_of((group * group_occ + i) * vir_count, vir_count)
            term = lax.dot_general(
                rear[slot, i * width : (i + 1) * width, :],
                cf[:, pl.ds(start, vir_count)],
                (((1,), (1,)), ((), ())),
                preferred_element_type=f32,
            )
            total = term if total is None else total + term
        factored[...] = total if slot == 0 else factored[...] + total

    base1, base2 = nz, 2 * nz
    for n in near[::-1]:
        push(n, own, at(g, lax.rem(z + n, nz), y, v))
    push(base1, own, p1)
    push(base2, own, p2)
    push_twin(0, 0, own)
    loads[0].wait()
    for k in range(2 * nz):
        for t in range(batches):
            occ_float[k, :, t * part : (t + 1) * part] = occ[
                t, k * group_occ : (k + 1) * group_occ, :
            ].astype(f32)

    def second(n):
        j = block(g1, n, y1)
        arrive(base1 + n, j)
        push(base2 + nz + n, j, p2)
        push_twin(kind1, n, j)
        j = block(g2, n, y2)
        arrive(base2 + n, j)
        push_twin(kind2, n, j)

    second(0)
    for n in near:
        j = block(g, n, y)
        arrive(n, j)
        push(base1 + n, j, p1)
        push(base2 + n, j, p2)
        push_twin(0, n, j)
    loads[1].wait()
    loads[2].wait()
    for k, n in enumerate(order):
        if k > 0:
            second(n)
            absorb(g, 0, order[k - 1], k - 1)
    for k, n in enumerate(order):
        j = block(g3, n, y3)
        arrive(base2 + nz + n, j)
        push_twin(3, n, j)
        if k == 0:
            absorb(g, 0, order[-1], nz - 1)
        else:
            absorb(g3, 1, order[k - 1], nz + k - 1)
    absorb(g3, 1, order[-1], 2 * nz - 1)

    weights = weight_ref[:, pl.ds(first_slot, part)]
    place = first_slot + lax.broadcasted_iota(jnp.int32, (1, part), 1)
    for t in range(batches):
        span = slice(t * part, (t + 1) * part)
        weight = jnp.where(place < live_ref[t], weights[t : t + 1, :], 0.0)
        density[:, span] = density[:, span] * weight
    doubled = (2.0 * factored[...].astype(bf16).astype(f32)).astype(bf16)

    def terms(gg, n):
        group = gg * nz + zed(n)
        pieces = []
        for t in range(batches):
            span = slice(t * part, (t + 1) * part)
            o = occ_float[group, :, span]
            pieces.append(
                (o[:, None, :] * density[:, span][None, :, :]).reshape(lines, part).astype(bf16)
            )
        exchange = jnp.dot(
            jnp.concatenate(pieces, axis=1),
            vir[...].reshape(points, vir_count),
            preferred_element_type=f32,
        )
        for i in range(group_occ):
            start = pl.multiple_of((group * group_occ + i) * vir_count, vir_count)
            both = exchange[i * width : (i + 1) * width, :] + jnp.dot(
                doubled, cf[:, pl.ds(start, vir_count)], preferred_element_type=f32
            )
            for c in range(per_occ):
                m = i * per_occ + c
                partial[group * 2 + m // (2 * chunks), (m // chunks) % 2, m % chunks] = both[
                    :, c * LANES : (c + 1) * LANES
                ]

    far = near[::-1] + [0]
    drain = []

    def twin_copy(kind, n, j, vv):
        return pltpu.make_async_remote_copy(
            src_ref=partial.at[j, vv],
            dst_ref=land_d.at[j],
            send_sem=rd_send.at[kind * nz + n],
            recv_sem=rd_recv.at[kind * nz + n],
            device_id=twin,
            device_id_type=MESH,
        )

    def wire(src, dst, slot, index, peer):
        return pltpu.make_async_remote_copy(
            src_ref=src.at[slot],
            dst_ref=dst.at[slot],
            send_sem=rs_send.at[index],
            recv_sem=rs_recv.at[index],
            device_id=peer,
            device_id_type=MESH,
        )

    def pair_sum(kind, n, j):
        twin_copy(kind, n, j, 1 - v).wait_recv()
        return partial[j, v] + land_d[j]

    def give(copy):
        copy.start()
        drain.append(copy)

    def stage_a(n):
        for half, (kind, gg, yy) in enumerate(((3, g3, y3), (kind2, g2, y2))):
            k = half * nz + n
            send_a[k] = pair_sum(kind, n, block(gg, n, yy)).astype(bf16)
            give(wire(send_a, land_a, k, k, p2))

    for k, n in enumerate(far):
        for fx, gg in ((1, g3), (0, g)):
            terms(gg, n)
            for fy, yy in ((1, y3), (0, y)):
                give(twin_copy(2 * fx + fy, n, block(gg, n, yy), 1 - v))
            if fx == 1 and k > 0:
                stage_a(far[k - 1])
    stage_a(far[-1])
    for n in far:
        total = pair_sum(kind1, n, block(g1, n, y1))
        wire(send_a, land_a, n, n, p2).wait_recv()
        send_b[n] = (total + land_a[n].astype(f32)).astype(bf16)
        give(wire(send_b, land_b, n, 2 * nz + n, p1))
    for n in far:
        total = pair_sum(0, n, block(g, n, y))
        wire(send_a, land_a, nz + n, nz + n, p2).wait_recv()
        total = total + land_a[nz + n].astype(f32)
        wire(send_b, land_b, n, 2 * nz + n, p1).wait_recv()
        total = total + land_b[n].astype(f32)
        if n > 0:
            send_z[n - 1] = total.astype(bf16)
            give(wire(send_z, land_z, n - 1, 3 * nz + n, at(g, zed(n), y, v)))
    for n in near:
        wire(send_z, land_z, n - 1, 3 * nz + n, p1).wait_recv()
        total = total + land_z[n - 1].astype(f32)
    for c in range(chunks):
        out_ref[:, c * LANES : (c + 1) * LANES] = total[c]
    for copy in sent + drain:
        copy.wait_send()


def fused_local(
    blk, trial, energy_gap, coulomb_factors, occ_values, vir_values, kernel, live_points
):
    pairs, width = trial.shape
    blocks = 2 * blk
    nz = blk // 2
    chunks = pairs // LANES
    batches, occ_count, batch_size = occ_values.shape
    vir_count = vir_values.shape[2]
    part = batch_size // 4
    cf_rows = coulomb_factors.shape[0] // 4
    group_occ = occ_count // blk
    bf16, f32 = jnp.bfloat16, jnp.float32
    vmem = pl.BlockSpec(memory_space=pltpu.VMEM)
    anywhere = pl.BlockSpec(memory_space=pl.ANY)
    dma = pltpu.SemaphoreType.DMA
    total = pl.pallas_call(
        functools.partial(fused_kernel, nz),
        out_shape=jax.ShapeDtypeStruct((width, pairs), f32),
        in_specs=[
            anywhere,
            anywhere,
            anywhere,
            anywhere,
            vmem,
            pl.BlockSpec(memory_space=pltpu.SMEM),
        ],
        out_specs=vmem,
        scratch_shapes=[
            pltpu.VMEM((blocks, 2, chunks, width, LANES), bf16),
            pltpu.VMEM((2 * nz, group_occ * width, vir_count), bf16),
            pltpu.VMEM((cf_rows, coulomb_factors.shape[1]), bf16),
            pltpu.VMEM((batches, occ_count, part), bf16),
            pltpu.VMEM((2 * nz, group_occ, batches * part), f32),
            pltpu.VMEM((batches, part, vir_count), bf16),
            pltpu.VMEM((width, batches * part), f32),
            pltpu.VMEM((width, cf_rows), f32),
            pltpu.VMEM((blocks, 2, chunks, width, LANES), f32),
            pltpu.VMEM((blocks, chunks, width, LANES), f32),
            pltpu.VMEM((2 * nz, chunks, width, LANES), bf16),
            pltpu.VMEM((2 * nz, chunks, width, LANES), bf16),
            pltpu.VMEM((nz, chunks, width, LANES), bf16),
            pltpu.VMEM((nz, chunks, width, LANES), bf16),
            pltpu.VMEM((nz, chunks, width, LANES), bf16),
            pltpu.VMEM((nz, chunks, width, LANES), bf16),
            dma((chunks,)),
            dma((3,)),
            dma((4 * nz,)),
            dma((4 * nz,)),
            dma((4 * nz,)),
            dma((4 * nz,)),
            dma((4 * nz,)),
            dma((4 * nz,)),
            dma((4 * nz,)),
            dma((4 * nz,)),
        ],
        compiler_params=pltpu.CompilerParams(
            collective_id=0, has_side_effects=True, vmem_limit_bytes=56 * 1024 * 1024
        ),
    )(trial.T, coulomb_factors, occ_values, vir_values, kernel, live_points)
    result = energy_gap[:, None] * trial.astype(f32) + total.T
    return result.astype(bf16)


def fits(mesh):
    def check(trial, coulomb_factors, occ_values, vir_values):
        return (
            mesh.shape["grp"] == 2
            and mesh.shape["vec"] == 2
            and mesh.shape["blk"] % 4 == 0
            and trial.shape[0] % LANES == 0
            and coulomb_factors.shape[0] % (4 * LANES) == 0
            and occ_values.shape[2] % (4 * LANES) == 0
            and occ_values.shape[1] % mesh.shape["blk"] == 0
            and vir_values.shape[2] % LANES == 0
        )

    return check


def solution(mesh):
    in_specs = (
        P(("grp", "blk", "vec"), None),
        P(("grp", "blk", "vec")),
        P("blk", None),
        P("blk", None, None),
        P("blk", None, None),
        P("blk", None),
        P("blk"),
    )
    out_specs = P(("grp", "blk", "vec"), None)
    check = fits(mesh)

    def local(trial, energy_gap, coulomb_factors, occ_values, vir_values, kernel, live_points):
        args = (trial, energy_gap, coulomb_factors, occ_values, vir_values, kernel, live_points)
        if check(trial, coulomb_factors, occ_values, vir_values):
            return fused_local(mesh.shape["blk"], *args)
        return collective_local(*args)

    return jax.shard_map(local, mesh=mesh, in_specs=in_specs, out_specs=out_specs, check_vma=False)
```

time: 47.8 us -> 40.3 us (0.84)
  Pallas kernels: 44.8 us -> 38.5 us
  local copies, waits for them, and re-layouts: 2.67 us -> 0.01 us
  other arithmetic: 0 us -> 1.52 us
    pallas_call x1, Pallas kernels: 44.8 us -> 38.5 us  [fused_local(): pl.pallas_call(functools.partial(fused_kernel, nz), out_shape=jax.ShapeDt...]
    convert_element_type x0 -> x1, other arithmetic: none -> 1.52 us  [fused_local(): return result.astype(bf16)]
    unnamed x1 -> x4, local copies, waits for them, and re-layouts: 1.4 us -> 0.01 us
    broadcast_in_dim x1 -> x0, local copies, waits for them, and re-layouts: 1.27 us -> none  [fused_local(): energy_gap[None, :]]
where the time goes in v2:
time: 40.3 us; the launch traced here: 40.1 us
  Pallas kernels  38.5 us (96%)
  other arithmetic  1.52 us (4%)
    pallas_call x1, Pallas kernels, fused_local(): pl.pallas_call(functools.partial(fused_kernel, nz), out_shape=jax.ShapeDt...  38.5 us
    convert_element_type x1, other arithmetic, fused_local(): return result.astype(bf16)  1.52 us

profile of v2, /device:TPU:0, one launch (start us, length us, event | category | flops | bytes accessed | tf_op | source)
XLA Modules:
  0.0 40.1 jit_solution(1965023318612667776)
XLA Ops:
  0.0 0.0 copy-start
  0.0 0.0 copy-start.1
  0.0 38.5 %shard_map.73 = f32[32,640]{1,0:T(8,128)} custom-call(bf16[32,640]{1,0:T(8,128)(2,1)} %bitcast.5, bf16[512,20480]{1,0:T(8,128)(2,1)} %cf_hbm.1, bf16[10,40,512]{2,1,0:T(8,128)(2,1)} %occ_hbm.1, bf16[10,512,512]{2,1,0:T(8,128)(2,1)} %vir_hbm.1, f32[10,512]{1,0:T(8,128)} %weight_ref.1, s32[10]{0:T(128)} %live_ref.1), custom_call_target="tpu_custom_call" | custom-call | tf_op jit(solution)/shard_map/pallas_call | solution.py:415
  38.5 0.0 copy-done
  38.6 0.0 copy-done.1
  38.6 1.5 %fusion = bf16[640,32]{0,1:T(8,128)(2,1)} fusion(f32[32,640]{1,0:T(8,128)} %shard_map.73, bf16[640,32]{0,1:T(8,128)(2,1)S(1)} %copy-done, f32[640]{0:T(1024)S(1)} %copy-done.1), kind=kLoop, calls=%fused_computation.1 | loop fusion | flops 81920 | bytes 166400 | tf_op jit(solution)/shard_map/convert_element_type | solution.py:460
Async XLA Ops:
  0.0 38.5 %copy-start = (bf16[640,32]{0,1:T(8,128)(2,1)S(1)}, bf16[640,32]{0,1:T(8,128)(2,1)}, u32[]{:S(2)}) copy-start(bf16[640,32]{0,1:T(8,128)(2,1)} %param.7) | copy-start | bytes 122884
  0.0 38.6 %copy-start.1 = (f32[640]{0:T(1024)S(1)}, f32[640]{0:T(1024)}, u32[]{:S(2)}) copy-start(f32[640]{0:T(1024)} %param.8) | copy-start | bytes 7684

commit v3 on v2

--- a/solution.py
+++ b/solution.py
@@ -144,7 +144,11 @@
     step = 2 if batches % 2 == 0 else 1
 
     def zed(n):
-        return lax.rem(z + nz - n, nz)
+        other = z
+        for k in range(nz.bit_length() - 1):
+            if n >> k & 1:
+                other = other + (1 - 2 * lax.rem(z // 2**k, 2)) * 2**k
+        return other
 
     def block(gg, n, yy):
         return gg * (2 * nz) + zed(n) * 2 + yy
@@ -188,7 +192,7 @@
         copy.wait()
     pl.semaphore_wait(barrier, len(peers))
 
-    near = sorted(range(1, nz), key=lambda n: min(n, nz - n))
+    near = list(range(1, nz))
     order = [0] + near
     sent = []
 
@@ -251,8 +255,8 @@
         factored[...] = total if slot == 0 else factored[...] + total
 
     base1, base2 = nz, 2 * nz
-    for n in near[::-1]:
-        push(n, own, at(g, lax.rem(z + n, nz), y, v))
+    for n in near:
+        push(n, own, at(g, zed(n), y, v))
     push(base1, own, p1)
     push(base2, own, p2)
     push_twin(0, 0, own)
@@ -328,7 +332,7 @@
                     :, c * LANES : (c + 1) * LANES
                 ]
 
-    far = near[::-1] + [0]
+    last_own = near + [0]
     drain = []
 
     def twin_copy(kind, n, j, vv):
@@ -365,20 +369,20 @@
             send_a[k] = pair_sum(kind, n, block(gg, n, yy)).astype(bf16)
             give(wire(send_a, land_a, k, k, p2))
 
-    for k, n in enumerate(far):
+    for k, n in enumerate(last_own):
         for fx, gg in ((1, g3), (0, g)):
             terms(gg, n)
             for fy, yy in ((1, y3), (0, y)):
                 give(twin_copy(2 * fx + fy, n, block(gg, n, yy), 1 - v))
             if fx == 1 and k > 0:
-                stage_a(far[k - 1])
-    stage_a(far[-1])
-    for n in far:
+                stage_a(last_own[k - 1])
+    stage_a(last_own[-1])
+    for n in last_own:
         total = pair_sum(kind1, n, block(g1, n, y1))
         wire(send_a, land_a, n, n, p2).wait_recv()
         send_b[n] = (total + land_a[n].astype(f32)).astype(bf16)
         give(wire(send_b, land_b, n, 2 * nz + n, p1))
-    for n in far:
+    for n in last_own:
         total = pair_sum(0, n, block(g, n, y))
         wire(send_a, land_a, nz + n, nz + n, p2).wait_recv()
         total = total + land_a[nz + n].astype(f32)
@@ -466,6 +470,7 @@
             mesh.shape["grp"] == 2
             and mesh.shape["vec"] == 2
             and mesh.shape["blk"] % 4 == 0
+            and mesh.shape["blk"] & (mesh.shape["blk"] - 1) == 0
             and trial.shape[0] % LANES == 0
             and coulomb_factors.shape[0] % (4 * LANES) == 0
             and occ_values.shape[2] % (4 * LANES) == 0

time: 40.3 us -> 39.2 us (0.973)
  Pallas kernels: 38.5 us -> 37.4 us
    pallas_call x1, Pallas kernels: 38.5 us -> 37.4 us  [fused_local(): pl.pallas_call(functools.partial(fused_kernel, nz), out_shape=jax.ShapeDt...]
where the time goes in v3:
time: 39.2 us; the launch traced here: 39 us
  Pallas kernels  37.4 us (95%)
  other arithmetic  1.52 us (4%)
    pallas_call x1, Pallas kernels, fused_local(): pl.pallas_call(functools.partial(fused_kernel, nz), out_shape=jax.ShapeDt...  37.4 us
    convert_element_type x1, other arithmetic, fused_local(): return result.astype(bf16)  1.52 us

profile of v3, /device:TPU:0, one launch (start us, length us, event | category | flops | bytes accessed | tf_op | source)
XLA Modules:
  0.0 39.0 jit_solution(8579454619438479014)
XLA Ops:
  0.0 0.0 copy-start
  0.0 0.0 copy-start.1
  0.0 37.4 %shard_map.73 = f32[32,640]{1,0:T(8,128)} custom-call(bf16[32,640]{1,0:T(8,128)(2,1)} %bitcast.5, bf16[512,20480]{1,0:T(8,128)(2,1)} %cf_hbm.1, bf16[10,40,512]{2,1,0:T(8,128)(2,1)} %occ_hbm.1, bf16[10,512,512]{2,1,0:T(8,128)(2,1)} %vir_hbm.1, f32[10,512]{1,0:T(8,128)} %weight_ref.1, s32[10]{0:T(128)} %live_ref.1), custom_call_target="tpu_custom_call" | custom-call | tf_op jit(solution)/shard_map/pallas_call | solution.py:419
  37.5 0.0 copy-done
  37.5 0.0 copy-done.1
  37.5 1.5 %fusion = bf16[640,32]{0,1:T(8,128)(2,1)} fusion(f32[32,640]{1,0:T(8,128)} %shard_map.73, bf16[640,32]{0,1:T(8,128)(2,1)S(1)} %copy-done, f32[640]{0:T(1024)S(1)} %copy-done.1), kind=kLoop, calls=%fused_computation.1 | loop fusion | flops 81920 | bytes 166400 | tf_op jit(solution)/shard_map/convert_element_type | solution.py:464
Async XLA Ops:
  0.0 37.5 %copy-start = (bf16[640,32]{0,1:T(8,128)(2,1)S(1)}, bf16[640,32]{0,1:T(8,128)(2,1)}, u32[]{:S(2)}) copy-start(bf16[640,32]{0,1:T(8,128)(2,1)} %param.7) | copy-start | bytes 122884
  0.0 37.5 %copy-start.1 = (f32[640]{0:T(1024)S(1)}, f32[640]{0:T(1024)}, u32[]{:S(2)}) copy-start(f32[640]{0:T(1024)} %param.8) | copy-start | bytes 7684

commit v4 on v3

--- a/solution.py
+++ b/solution.py
@@ -369,6 +369,12 @@
             send_a[k] = pair_sum(kind, n, block(gg, n, yy)).astype(bf16)
             give(wire(send_a, land_a, k, k, p2))
 
+    def stage_b(n):
+        total = pair_sum(kind1, n, block(g1, n, y1))
+        wire(send_a, land_a, n, n, p2).wait_recv()
+        send_b[n] = (total + land_a[n].astype(f32)).astype(bf16)
+        give(wire(send_b, land_b, n, 2 * nz + n, p1))
+
     for k, n in enumerate(last_own):
         for fx, gg in ((1, g3), (0, g)):
             terms(gg, n)
@@ -376,12 +382,11 @@
                 give(twin_copy(2 * fx + fy, n, block(gg, n, yy), 1 - v))
             if fx == 1 and k > 0:
                 stage_a(last_own[k - 1])
+            if fx == 0 and k > 1:
+                stage_b(last_own[k - 2])
     stage_a(last_own[-1])
-    for n in last_own:
-        total = pair_sum(kind1, n, block(g1, n, y1))
-        wire(send_a, land_a, n, n, p2).wait_recv()
-        send_b[n] = (total + land_a[n].astype(f32)).astype(bf16)
-        give(wire(send_b, land_b, n, 2 * nz + n, p1))
+    for n in last_own[-2:]:
+        stage_b(n)
     for n in last_own:
         total = pair_sum(0, n, block(g, n, y))
         wire(send_a, land_a, nz + n, nz + n, p2).wait_recv()

time: 39.2 us -> 39.6 us (1.010)
  Pallas kernels: 37.4 us -> 37.9 us
    pallas_call x1, Pallas kernels: 37.4 us -> 37.9 us  [fused_local(): pl.pallas_call(functools.partial(fused_kernel, nz), out_shape=jax.ShapeDt...]
where the time goes in v4:
time: 39.6 us; the launch traced here: 39.4 us
  Pallas kernels  37.9 us (96%)
  other arithmetic  1.52 us (4%)
    pallas_call x1, Pallas kernels, fused_local(): pl.pallas_call(functools.partial(fused_kernel, nz), out_shape=jax.ShapeDt...  37.9 us
    convert_element_type x1, other arithmetic, fused_local(): return result.astype(bf16)  1.52 us

profile of v4, /device:TPU:0, one launch (start us, length us, event | category | flops | bytes accessed | tf_op | source)
XLA Modules:
  0.0 39.4 jit_solution(7318454836260627610)
XLA Ops:
  0.0 0.0 copy-start
  0.0 0.0 copy-start.1
  0.0 37.9 %shard_map.73 = f32[32,640]{1,0:T(8,128)} custom-call(bf16[32,640]{1,0:T(8,128)(2,1)} %bitcast.5, bf16[512,20480]{1,0:T(8,128)(2,1)} %cf_hbm.1, bf16[10,40,512]{2,1,0:T(8,128)(2,1)} %occ_hbm.1, bf16[10,512,512]{2,1,0:T(8,128)(2,1)} %vir_hbm.1, f32[10,512]{1,0:T(8,128)} %weight_ref.1, s32[10]{0:T(128)} %live_ref.1), custom_call_target="tpu_custom_call" | custom-call | tf_op jit(solution)/shard_map/pallas_call | solution.py:424
  37.9 0.0 copy-done
  37.9 0.0 copy-done.1
  37.9 1.5 %fusion = bf16[640,32]{0,1:T(8,128)(2,1)} fusion(f32[32,640]{1,0:T(8,128)} %shard_map.73, bf16[640,32]{0,1:T(8,128)(2,1)S(1)} %copy-done, f32[640]{0:T(1024)S(1)} %copy-done.1), kind=kLoop, calls=%fused_computation.1 | loop fusion | flops 81920 | bytes 166400 | tf_op jit(solution)/shard_map/convert_element_type | solution.py:469
Async XLA Ops:
  0.0 37.9 %copy-start = (bf16[640,32]{0,1:T(8,128)(2,1)S(1)}, bf16[640,32]{0,1:T(8,128)(2,1)}, u32[]{:S(2)}) copy-start(bf16[640,32]{0,1:T(8,128)(2,1)} %param.7) | copy-start | bytes 122884
  0.0 37.9 %copy-start.1 = (f32[640]{0:T(1024)S(1)}, f32[640]{0:T(1024)}, u32[]{:S(2)}) copy-start(f32[640]{0:T(1024)} %param.8) | copy-start | bytes 7684
